TPU v7x, 8 devices: a whole 2x2x1 slice. The times are simulated.
8 devices in a mesh: dp: 1 (over z), cp: 8 (over y, x, core).
Axes of the slice: x: 2, y: 2, z: 1, core: 2. Of those that a mesh axis runs over, the one named last changes fastest.
Arguments:
- hidden: bfloat16 [8, 1024, 3840], P('dp', 'cp')
- grad_out: bfloat16 [8, 1024, 3840], P('dp', 'cp')
- norm_gain: float32 [2, 3840], replicated
- w_qkv: bfloat16 [2, 3840, 8192], replicated
- b_qkv: float32 [2, 8192], replicated
- w_out: bfloat16 [2, 4096, 3840], replicated
- b_out: float32 [2, 3840], replicated
- attn_sinks: float32 [2, 16], replicated
Outputs:
- output 1: bfloat16 [8, 1024, 3840], P('dp', 'cp')
- output 2: bfloat16 [8, 1024, 3840], P('dp', 'cp')
- output 3: float32 [8, 2, 3840], P(('dp', 'cp'))
- output 4: float32 [8, 2, 8192], P(('dp', 'cp'))
- output 5: float32 [8, 2, 3840], P(('dp', 'cp'))
- output 6: float32 [8, 2, 16], P(('dp', 'cp'))
All inputs are finite; a program needn't handle non-finite values.
Results may differ from a plain program's by a relative error of at most 0.02.
Values are sent between devices in bfloat16 or wider.
A program may use at most 1 GiB of HBM per device.

v0:
```python
import jax
import jax.numpy as jnp
import math
from jax import lax
from jax.sharding import PartitionSpec as P

WINDOW = 128
EPSILON = 1e-5
ROPE_THETA = 150000.0
YARN_FACTOR = 32.0
YARN_CONTEXT = 4096.0
YARN_ALPHA = 1.0
YARN_BETA = 32.0


def rope_tables(positions, head_dim):
    half_dim = head_dim // 2
    freq_steps = jnp.arange(half_dim, dtype=jnp.float32)
    freq_base = ROPE_THETA ** (freq_steps * 2.0 / head_dim)
    concentration = 0.1 * math.log(YARN_FACTOR) + 1.0
    low_edge = half_dim * math.log(YARN_CONTEXT / (YARN_BETA * 2.0 * math.pi)) / math.log(ROPE_THETA)
    high_edge = half_dim * math.log(YARN_CONTEXT / (YARN_ALPHA * 2.0 * math.pi)) / math.log(ROPE_THETA)
    ramp_pos = jnp.clip((freq_steps - low_edge) / (high_edge - low_edge), 0.0, 1.0)
    inv_freq = (1.0 - ramp_pos) / freq_base + ramp_pos / (YARN_FACTOR * freq_base)
    angles = positions.astype(jnp.float32)[:, None] * inv_freq[None, :]
    return jnp.cos(angles) * concentration, jnp.sin(angles) * concentration


def rotate_half(tensor, cos_tab, sin_tab):
    half_dim = tensor.shape[-1] // 2
    first_half = tensor[..., :half_dim]
    second_half = tensor[..., half_dim:]
    return jnp.concatenate([first_half * cos_tab - second_half * sin_tab, second_half * cos_tab + first_half * sin_tab], axis=-1)


def norm_project(hid_f, gain_row, w_in, bias_row, cos_tab, sin_tab, num_heads, kv_heads):
    batch_size, seq_dev = hid_f.shape[0], hid_f.shape[1]
    head_dim = 2 * cos_tab.shape[-1]
    q_width = num_heads * head_dim
    k_width = kv_heads * head_dim
    inv_rms = lax.rsqrt(jnp.mean(hid_f * hid_f, axis=-1, keepdims=True) + EPSILON)
    normed = (hid_f * inv_rms * gain_row).astype(jnp.bfloat16)
    projected = jnp.dot(normed, w_in, preferred_element_type=jnp.float32) + bias_row
    query_rows = rotate_half(projected[..., :q_width].reshape(batch_size, seq_dev, kv_heads, num_heads // kv_heads, head_dim), cos_tab[:, None, None, :], sin_tab[:, None, None, :])
    key_rows = rotate_half(projected[..., q_width:q_width + k_width].reshape(batch_size, seq_dev, kv_heads, head_dim), cos_tab[:, None, :], sin_tab[:, None, :])
    value_rows = projected[..., q_width + k_width:].reshape(batch_size, seq_dev, kv_heads, head_dim)
    return query_rows.astype(jnp.bfloat16), key_rows.astype(jnp.bfloat16), value_rows.astype(jnp.bfloat16), inv_rms


def attend_forward(query_rows, key_rows, value_rows, sink_row, row_pos, key_pos, window_on, logit_scale):
    kv_heads, group_size = query_rows.shape[2], query_rows.shape[3]
    scores = jnp.einsum('bqkgd,bskd->bkgqs', query_rows, key_rows, preferred_element_type=jnp.float32) * logit_scale
    key_mask = (key_pos[None, :] <= row_pos[:, None]) & (key_pos[None, :] >= 0)
    if window_on:
        key_mask = key_mask & (key_pos[None, :] >= row_pos[:, None] - WINDOW)
    scores = jnp.where(key_mask, scores, -jnp.inf)
    sink_grid = sink_row.reshape(kv_heads, group_size)[None, :, :, None]
    row_peak = jnp.maximum(jnp.max(scores, axis=-1), sink_grid)
    exp_scores = jnp.exp(scores - row_peak[..., None])
    sink_exp = jnp.exp(sink_grid - row_peak)
    denominator = jnp.sum(exp_scores, axis=-1) + sink_exp
    prob_f32 = exp_scores / denominator[..., None]
    prob_bf = prob_f32.astype(jnp.bfloat16)
    attn_out = jnp.einsum('bkgqs,bskd->bqkgd', prob_bf, value_rows, preferred_element_type=jnp.float32).astype(jnp.bfloat16)
    return attn_out, prob_f32, prob_bf, sink_exp / denominator


def attend_backward(d_attn, query_rows, key_rows, value_rows, prob_f32, prob_bf, sink_prob, logit_scale):
    d_prob = jnp.einsum('bqkgd,bskd->bkgqs', d_attn, value_rows, preferred_element_type=jnp.float32).astype(jnp.bfloat16).astype(jnp.float32)
    row_delta = jnp.sum(prob_f32 * d_prob, axis=-1)
    d_scores = (prob_f32 * (d_prob - row_delta[..., None])).astype(jnp.bfloat16)
    d_query = (jnp.einsum('bkgqs,bskd->bqkgd', d_scores, key_rows, preferred_element_type=jnp.float32) * logit_scale).astype(jnp.bfloat16)
    d_keys = jnp.einsum('bkgqs,bqkgd->bskd', d_scores, query_rows, preferred_element_type=jnp.float32) * logit_scale
    d_values = jnp.einsum('bkgqs,bqkgd->bskd', prob_bf, d_attn, preferred_element_type=jnp.float32)
    d_sink = -jnp.sum(sink_prob * row_delta, axis=(0, 3)).reshape(-1)
    return d_query, d_keys, d_values, d_sink


def project_backward(d_query, d_keys, d_values, hid_f, inv_rms, gain_row, w_in, cos_tab, sin_tab):
    batch_size, seq_dev = hid_f.shape[0], hid_f.shape[1]
    dq_rot = rotate_half(d_query.astype(jnp.float32), cos_tab[:, None, None, :], -sin_tab[:, None, None, :]).reshape(batch_size, seq_dev, -1)
    dk_rot = rotate_half(d_keys.astype(jnp.float32), cos_tab[:, None, :], -sin_tab[:, None, :]).reshape(batch_size, seq_dev, -1)
    d_proj = jnp.concatenate([dq_rot, dk_rot, d_values.astype(jnp.float32).reshape(batch_size, seq_dev, -1)], axis=-1)
    d_bias = jnp.sum(d_proj, axis=(0, 1))
    d_normed = jnp.einsum('bsq,dq->bsd', d_proj.astype(jnp.bfloat16), w_in, preferred_element_type=jnp.float32).astype(jnp.bfloat16).astype(jnp.float32)
    d_gain = jnp.sum(d_normed * hid_f * inv_rms, axis=(0, 1))
    unit_grad = d_normed * gain_row
    d_hid = inv_rms * unit_grad - hid_f * inv_rms ** 3 * jnp.mean(unit_grad * hid_f, axis=-1, keepdims=True)
    return d_hid, d_gain, d_bias


def dense_out(attn_out, w_proj, bias_row):
    batch_size, seq_dev = attn_out.shape[0], attn_out.shape[1]
    return jnp.dot(attn_out.reshape(batch_size, seq_dev, -1), w_proj, preferred_element_type=jnp.float32) + bias_row


def solution(mesh):
    num_shards = mesh.shape['cp']
    forward_pairs = [(source, source + 1) for source in range(num_shards - 1)]
    backward_pairs = [(source + 1, source) for source in range(num_shards - 1)]
    row_spec = P('dp', 'cp')
    device_spec = P(('dp', 'cp'))
    whole_spec = P()

    def local_step(hidden, grad_out, norm_gain, w_qkv, b_qkv, w_out, b_out, attn_sinks):
        seq_dev = hidden.shape[1]
        num_heads = attn_sinks.shape[1]
        head_dim = w_out.shape[1] // num_heads
        kv_heads = (w_qkv.shape[2] // head_dim - num_heads) // 2
        logit_scale = head_dim ** -0.5
        shard_start = lax.axis_index('cp') * seq_dev
        row_pos = shard_start + jnp.arange(seq_dev)
        cos_tab, sin_tab = rope_tables(row_pos, head_dim)

        hid_one = hidden.astype(jnp.float32)
        query_one, keys_one, values_one, rms_one = norm_project(hid_one, norm_gain[0], w_qkv[0], b_qkv[0], cos_tab, sin_tab, num_heads, kv_heads)
        tail_rows = jnp.concatenate([keys_one[:, seq_dev - WINDOW:], values_one[:, seq_dev - WINDOW:]], axis=2)
        prev_rows = lax.ppermute(tail_rows, 'cp', forward_pairs)
        near_keys = jnp.concatenate([prev_rows[:, :, :kv_heads], keys_one], axis=1)
        near_values = jnp.concatenate([prev_rows[:, :, kv_heads:], values_one], axis=1)
        near_pos = jnp.concatenate([shard_start - WINDOW + jnp.arange(WINDOW), row_pos])
        attn_one, prob_one, probbf_one, sink_one = attend_forward(query_one, near_keys, near_values, attn_sinks[0], row_pos, near_pos, True, logit_scale)
        middle = (hid_one + dense_out(attn_one, w_out[0], b_out[0])).astype(jnp.bfloat16)

        hid_two = middle.astype(jnp.float32)
        query_two, keys_two, values_two, rms_two = norm_project(hid_two, norm_gain[1], w_qkv[1], b_qkv[1], cos_tab, sin_tab, num_heads, kv_heads)
        all_rows = lax.all_gather(jnp.concatenate([keys_two, values_two], axis=2), 'cp', axis=1, tiled=True)
        far_keys = all_rows[:, :, :kv_heads]
        far_values = all_rows[:, :, kv_heads:]
        far_pos = jnp.arange(all_rows.shape[1])
        attn_two, prob_two, probbf_two, sink_two = attend_forward(query_two, far_keys, far_values, attn_sinks[1], row_pos, far_pos, False, logit_scale)
        output = (hid_two + dense_out(attn_two, w_out[1], b_out[1])).astype(jnp.bfloat16)

        d_out_two = grad_out.astype(jnp.float32)
        d_attn_two = jnp.einsum('bsd,qd->bsq', grad_out, w_out[1], preferred_element_type=jnp.float32).astype(jnp.bfloat16).reshape(query_two.shape)
        dq_two, dk_far, dv_far, dsink_two = attend_backward(d_attn_two, query_two, far_keys, far_values, prob_two, probbf_two, sink_two, logit_scale)
        own_two = lax.psum_scatter(jnp.concatenate([dk_far, dv_far], axis=2).astype(jnp.bfloat16), 'cp', scatter_dimension=1, tiled=True)
        dhid_two, dgain_two, dbias_two = project_backward(dq_two, own_two[:, :, :kv_heads], own_two[:, :, kv_heads:], hid_two, rms_two, norm_gain[1], w_qkv[1], cos_tab, sin_tab)
        d_middle = (d_out_two + dhid_two).astype(jnp.bfloat16)

        d_mid_f = d_middle.astype(jnp.float32)
        d_attn_one = jnp.einsum('bsd,qd->bsq', d_middle, w_out[0], preferred_element_type=jnp.float32).astype(jnp.bfloat16).reshape(query_one.shape)
        dq_one, dk_near, dv_near, dsink_one = attend_backward(d_attn_one, query_one, near_keys, near_values, prob_one, probbf_one, sink_one, logit_scale)
        near_grad = jnp.concatenate([dk_near, dv_near], axis=2)
        prev_grad = lax.ppermute(near_grad[:, :WINDOW].astype(jnp.bfloat16), 'cp', backward_pairs)
        own_grad = near_grad[:, WINDOW:]
        cut_row = seq_dev - WINDOW
        own_one = jnp.concatenate([own_grad[:, :cut_row], own_grad[:, cut_row:] + prev_grad.astype(jnp.float32)], axis=1).astype(jnp.bfloat16)
        dhid_one, dgain_one, dbias_one = project_backward(dq_one, own_one[:, :, :kv_heads], own_one[:, :, kv_heads:], hid_one, rms_one, norm_gain[0], w_qkv[0], cos_tab, sin_tab)
        d_hidden = (d_mid_f + dhid_one).astype(jnp.bfloat16)

        d_gain = jnp.stack([dgain_one, dgain_two])[None]
        d_bias_qkv = jnp.stack([dbias_one, dbias_two])[None]
        d_bias_out = jnp.stack([jnp.sum(d_mid_f, axis=(0, 1)), jnp.sum(d_out_two, axis=(0, 1))])[None]
        d_sinks = jnp.stack([dsink_one, dsink_two])[None]
        return output, d_hidden, d_gain, d_bias_qkv, d_bias_out, d_sinks

    return jax.shard_map(local_step, mesh=mesh, in_specs=(row_spec, row_spec, whole_spec, whole_spec, whole_spec, whole_spec, whole_spec, whole_spec), out_specs=(row_spec, row_spec, device_spec, device_spec, device_spec, device_spec), check_vma=False)
```

profile of v0, /device:TPU:7, one launch (start us, length us, event | category | flops | bytes accessed | tf_op | source)
XLA Modules:
  0.0 1960.8 jit_solution(11079348248808271080)
XLA Ops:
  16.3 74.6 %fusion.44 = f32[8,128,8192]{2,1,0:T(8,128)} fusion(bf16[2,3840,8192]{2,1,0:T(8,128)(2,1)} %param.11, f32[8192]{0:T(1024)S(1)} %bitcast.282, bf16[8,128,3840]{2,1,0:T(8,128)(2,1)} %param.8, f32[3840]{0:T(1024)S(1)} %get-tuple-element.13, f32[8,128]{1,0:T(8,128)S(1)} %get-tuple-element.52), kind=kOutput, calls=%fused_computation.75 | convolution fusion | flops 64448626688 | bytes 104385536 | tf_op jit(solution)/shard_map/dot_general | solution.py:43
  138.3 22.0 %reshape.363 = f32[8,128,8,2,256]{4,3,2,1,0:T(2,128)} reshape(f32[8,128,4096]{2,1,0:T(8,128)} %slice.191) | data formatting | bytes 33554432 | tf_op jit(solution)/shard_map/reshape | solution.py:44
  209.0 13.3 convolution_convert_fusion.1
  222.4 41.4 %fusion.74 = (f32[8,128]{1,0:T(8,128)S(1)}, bf16[8,128,3840]{2,1,0:T(8,128)(2,1)S(1)}) fusion(f32[3840]{0:T(1024)S(1)} %get-tuple-element.11, bf16[8,128,4096]{1,2,0:T(8,128)(2,1)} %bitcast.284, bf16[2,4096,3840]{2,1,0:T(8,128)(2,1)} %param.13, bf16[8,128,3840]{2,1,0:T(8,128)(2,1)} %param.8), kind=kOutput, calls=%fused_computation.111 | convolution fusion | flops 32239779840 | bytes 55593984 | tf_op jit(solution)/shard_map/dot_general | solution.py:94
  264.5 74.3 %fusion.47 = f32[8,128,8192]{2,1,0:T(8,128)} fusion(bf16[2,3840,8192]{2,1,0:T(8,128)(2,1)} %param.11, f32[8192]{0:T(1024)S(1)} %bitcast.281, bf16[8,128,3840]{2,1,0:T(8,128)(2,1)S(1)} %get-tuple-element.61, f32[3840]{0:T(1024)S(1)} %copy-done.34, f32[8,128]{1,0:T(8,128)S(1)} %get-tuple-element.54), kind=kOutput, calls=%fused_computation.76 | convolution fusion | flops 64448626688 | bytes 104385536 | tf_op jit(solution)/shard_map/dot_general | solution.py:43
  404.4 40.2 %fusion.108 = bf16[8,128,4096]{2,1,0:T(8,128)(2,1)} fusion(bf16[8,128,3840]{2,1,0:T(8,128)(2,1)} %param.9, bf16[2,4096,3840]{2,1,0:T(8,128)(2,1)} %param.13), kind=kOutput, calls=%fused_computation.148 | convolution fusion | flops 32216449024 | bytes 47710208 | tf_op jit(solution)/shard_map/bsd,qd->bsq/dot_general | solution.py:135
  468.2 17.4 copy.60
  524.2 216.1 %all-gather.2.cloned.1.call-done = bf16[8,1024,16,256]{3,1,2,0:T(8,128)(2,1)} async-done(((bf16[8,128,16,256]{3,1,2,0:T(8,128)(2,1)}), bf16[8,1024,16,256]{3,1,2,0:T(8,128)(2,1)}) %all-gather.2.cloned.1.call-update) | async-done | bytes 67108880 | tf_op jit(solution)/shard_map/all_gather | solution.py:127
  740.4 36.7 %fusion.18 = (f32[8,8,2,128]{3,2,1,0:T(2,128)S(1)}, f32[8,8,1024,128,2]{3,2,4,1,0:T(8,128)}) fusion(pred[128,1024]{0,1:T(8,128)(4,1)S(1)} %iota_compare_fusion, bf16[8,128,8,2,128]{4,1,3,2,0:T(8,128)(2,1)} %get-tuple-element.23, bf16[8,128,8,2,128]{4,1,3,2,0:T(8,128)(2,1)} %get-tuple-element.22, bf16[8,1024,16,256]{3,1,2,0:T(8,128)(2,1)} %all-gather.2.cloned.1.call-done), kind=kOutput, calls=%fused_computation.25 | convolution fusion | flops 8657027072 | bytes 109248512 | tf_op jit(solution)/shard_map/bqkgd,bskd->bkgqs/dot_general | solution.py:52
  777.1 21.4 %fusion.13 = f32[8,8,2,128]{3,2,1,0:T(2,128)S(1)} fusion(f32[8,8,1024,128,2]{3,2,4,1,0:T(8,128)} %get-tuple-element.63, f32[8,8,2,128]{3,2,1,0:T(2,128)S(1)} %broadcast_maximum_fusion, pred[128,1024]{0,1:T(8,128)(4,1)S(1)} %iota_compare_fusion), kind=kLoop, calls=%fused_computation.20 | loop fusion | flops 67092480 | bytes 67371008 | tf_op jit(solution)/shard_map/reduce_sum | solution.py:61
  798.6 38.4 %fusion.20 = bf16[8,1024,8,256]{3,1,2,0:T(8,128)(2,1)} fusion(bf16[8,128,8,2,256]{1,4,3,2,0:T(8,128)(2,1)} %bitcast.275, f32[8,8,1024,128,2]{3,2,4,1,0:T(8,128)} %get-tuple-element.63, f32[8,8,2,128]{3,2,1,0:T(2,128)S(1)} %fusion.120, f32[8,8,2,128]{3,2,1,0:T(2,128)S(1)} %broadcast_maximum_fusion, pred[128,1024]{0,1:T(8,128)(4,1)S(1)} %iota_compare_fusion), kind=kOutput, calls=%fused_computation.39 | convolution fusion | flops 8690597888 | bytes 109314048 | tf_op jit(solution)/shard_map/bkgqs,bqkgd->bskd/dot_general | solution.py:74
  837.1 47.1 %fusion.1 = (f32[8,8,2,128]{3,2,1,0:T(2,128)S(1)}, bf16[8,8,1024,128,2]{3,2,4,1,0:T(8,128)(2,1)}) fusion(f32[8,8,2,128]{3,2,1,0:T(2,128)S(1)} %fusion.120, f32[8,8,2,128]{3,2,1,0:T(2,128)S(1)} %broadcast_maximum_fusion, f32[8,8,1024,128,2]{3,2,4,1,0:T(8,128)} %get-tuple-element.63, pred[128,1024]{0,1:T(8,128)(4,1)S(1)} %iota_compare_fusion, ...), kind=kOutput, calls=%fused_computation.6 | convolution fusion | flops 8724135936 | bytes 142934016 | tf_op jit(solution)/shard_map/bqkgd,bskd->bkgqs/dot_general | solution.py:69
  884.2 43.3 %fusion.3 = bf16[8,8,2,128,1024]{3,4,2,1,0:T(8,128)(2,1)} fusion(bf16[8,8,1024,128,2]{3,2,4,1,0:T(8,128)(2,1)} %get-tuple-element.65, f32[8,8,2,128]{3,2,1,0:T(2,128)S(1)} %get-tuple-element.64, f32[8,8,2,128]{3,2,1,0:T(2,128)S(1)} %fusion.120, f32[8,8,2,128]{3,2,1,0:T(2,128)S(1)} %broadcast_maximum_fusion, f32[8,8,1024,128,2]{3,2,4,1,0:T(8,128)} %get-tuple-element.63, ...), kind=kLoop, calls=%fused_computation.8 | loop fusion | flops 134217728 | bytes 134545408 | tf_op jit(solution)/shard_map/convert_element_type | solution.py:71
  927.5 28.7 %fusion.19 = bf16[8,1024,8,256]{3,1,2,0:T(8,128)(2,1)} fusion(bf16[8,8,2,128,1024]{3,4,2,1,0:T(8,128)(2,1)} %fusion.3, bf16[8,128,8,2,128]{4,1,3,2,0:T(8,128)(2,1)} %get-tuple-element.23, bf16[8,128,8,2,128]{4,1,3,2,0:T(8,128)(2,1)} %get-tuple-element.22), kind=kOutput, calls=%fused_computation.38 | convolution fusion | flops 8640266240 | bytes 75497472 | tf_op jit(solution)/shard_map/bkgqs,bqkgd->bskd/dot_general | solution.py:73
  956.2 44.7 %pad_maximum_fusion = bf16[8,1024,16,256]{3,1,2,0:T(8,128)(2,1)} fusion(bf16[8,1024,8,256]{3,1,2,0:T(8,128)(2,1)} %fusion.20, bf16[8,1024,8,256]{3,1,2,0:T(8,128)(2,1)} %fusion.19), kind=kLoop, calls=%fused_computation | loop fusion | flops 33554432 | bytes 134217728 | tf_op jit(solution)/shard_map/concatenate | solution.py:137
  1001.0 31.3 %convert_bitcast_fusion.1 = f32[8,128,8,2,256]{4,1,3,2,0:T(8,128)} fusion(bf16[8,8,2,128,1024]{3,4,2,1,0:T(8,128)(2,1)} %fusion.3, bf16[8,1024,16,256]{3,1,2,0:T(8,128)(2,1)} %all-gather.2.cloned.1.call-done), kind=kOutput, calls=%fused_computation.93 | convolution fusion | flops 8602517504 | bytes 83886080 | tf_op jit(solution)/shard_map/bkgqs,bskd->bqkgd/dot_general | solution.py:72
  1045.8 16.4 copy.70
  1062.2 17.5 copy.79
  1079.6 39.3 %fusion.111 = bf16[8,8,256,2,128]{4,2,3,1,0:T(8,128)(2,1)} fusion(bf16[8,1024,16,256]{3,1,2,0:T(8,128)(2,1)} %all-gather.2.cloned.1.call-done, f32[8,8,1024,128,2]{3,2,4,1,0:T(8,128)} %get-tuple-element.63, f32[8,8,2,128]{3,2,1,0:T(2,128)S(1)} %fusion.120, f32[8,8,2,128]{3,2,1,0:T(2,128)S(1)} %broadcast_maximum_fusion, ...), kind=kOutput, calls=%fused_computation.149 | convolution fusion | flops 8678014976 | bytes 109314048 | tf_op jit(solution)/shard_map/bkgqs,bskd->bqkgd/dot_general | solution.py:64
  1119.0 256.2 %reduce-scatter.2.cloned.1.call-done = bf16[8,128,16,256]{3,1,2,0:T(8,128)(2,1)} async-done(((bf16[8,1024,16,256]{3,1,2,0:T(8,128)(2,1)}), bf16[8,128,16,256]{3,1,2,0:T(8,128)(2,1)}) %reduce-scatter.2.cloned.1.call-update) | async-done | bytes 8388624 | tf_op jit(solution)/shard_map/reduce_scatter | solution.py:137
  1432.2 85.4 %fusion.81 = (f32[3840]{0:T(1024)}, f32[8,128]{1,0:T(8,128)S(1)}, bf16[8,128,3840]{2,1,0:T(8,128)(2,1)}) fusion(bf16[8,128,3840]{2,1,0:T(8,128)(2,1)} %copy-done.5, f32[8,128]{1,0:T(8,128)S(1)} %copy-done.50, f32[3840]{0:T(1024)S(1)} %copy-done.35, bf16[2,3840,8192]{2,1,0:T(8,128)(2,1)} %param.11, f32[8,128,2048]{2,1,0:T(8,128)} %copy.81, ...), kind=kOutput, calls=%fused_computation.118 | convolution fusion | flops 64510226432 | bytes 112236544 | tf_op jit(solution)/shard_map/bsq,dq->bsd/dot_general | solution.py:85
  1517.6 14.6 convert_reduce_fusion
  1532.2 40.3 %fusion.105 = bf16[8,128,4096]{2,1,0:T(8,128)(2,1)} fusion(bf16[8,128,3840]{2,1,0:T(8,128)(2,1)} %get-tuple-element.17, bf16[2,4096,3840]{2,1,0:T(8,128)(2,1)} %param.13), kind=kOutput, calls=%fused_computation.147 | convolution fusion | flops 32216449024 | bytes 47710208 | tf_op jit(solution)/shard_map/bsd,qd->bsq/dot_general | solution.py:142
  1584.5 17.0 fusion.57
  1601.4 15.0 convolution_bitcast_fusion
  1616.4 13.4 fusion.59
  1629.8 13.9 fusion.56
  1659.0 41.8 %fusion.77 = bf16[8,128,3840]{2,1,0:T(8,128)(2,1)} fusion(bf16[8,128,3840]{2,1,0:T(8,128)(2,1)} %copy-done.5, bf16[8,128,4096]{1,2,0:T(8,128)(2,1)} %bitcast.283, bf16[2,4096,3840]{2,1,0:T(8,128)(2,1)} %param.13, f32[3840]{0:T(1024)S(1)} %copy-done.52), kind=kOutput, calls=%fused_computation.114 | convolution fusion | flops 32227983360 | bytes 55589888 | tf_op jit(solution)/shard_map/dot_general | solution.py:94
  1725.8 16.3 copy.86
  1742.2 17.5 copy.95
  1854.7 84.6 %fusion.73 = (f32[3840]{0:T(1024)S(1)}, f32[8,128]{1,0:T(8,128)S(1)}, bf16[8,128,3840]{2,1,0:T(8,128)(2,1)}) fusion(bf16[8,128,3840]{2,1,0:T(8,128)(2,1)} %param.8, f32[8,128]{1,0:T(8,128)S(1)} %copy-done.47, f32[3840]{0:T(1024)S(1)} %copy-done.37, bf16[2,3840,8192]{2,1,0:T(8,128)(2,1)} %param.11, f32[8,128,2048]{2,1,0:T(8,128)} %copy.97, ...), kind=kOutput, calls=%fused_computation.110 | convolution fusion | flops 64510226432 | bytes 112236544 | tf_op jit(solution)/shard_map/bsq,dq->bsd/dot_general | solution.py:85
  1940.6 13.2 fusion.65
  (215 shorter events, 452.3 us)
Async XLA Ops:
  7.2 733.2 %all-gather.2.cloned.1.call-start = ((), (), s32[]{:S(2)}) async-start(), calls=%async_computation.1 | async-start | bytes 75497472 | tf_op jit(solution)/shard_map/all_gather | solution.py:127
  13.2 77.7 %copy-start.46 = (f32[8,128]{1,0:T(8,128)}, f32[8,128]{1,0:T(8,128)S(1)}, u32[]{:S(2)}) copy-start(f32[8,128]{1,0:T(8,128)S(1)} %get-tuple-element.52) | copy-start | bytes 12292
  14.7 76.2 %copy-start.36 = (f32[3840]{0:T(1024)}, f32[3840]{0:T(1024)S(1)}, u32[]{:S(2)}) copy-start(f32[3840]{0:T(1024)S(1)} %get-tuple-element.13) | copy-start | bytes 46084
  118.3 53.2 %copy-start.6 = (f32[128,128]{1,0:T(8,128)}, f32[128,128]{1,0:T(8,128)S(1)}, u32[]{:S(2)}) copy-start(f32[128,128]{1,0:T(8,128)S(1)} %get-tuple-element.57) | copy-start | bytes 196612
  118.3 53.2 %copy-start.12 = (f32[128,128]{1,0:T(8,128)}, f32[128,128]{1,0:T(8,128)S(1)}, u32[]{:S(2)}) copy-start(f32[128,128]{1,0:T(8,128)S(1)} %get-tuple-element.56) | copy-start | bytes 196612
  124.6 55.0 %collective-permute-start = (bf16[8,128,16,256]{3,1,2,0:T(8,128)(2,1)}, bf16[8,128,16,256]{3,1,2,0:T(8,128)(2,1)}, u32[]{:S(2)}, u32[]{:S(2)}) collective-permute-start(bf16[8,128,16,256]{3,1,2,0:T(8,128)(2,1)} %pad_maximum_fusion.6), channel_id=1, source_target_pairs={{0,1},{1,2},{2,3},{3,4},{4,5},{5,6},{6,7}} | collective-permute-start | bytes 25165832 | tf_op jit(solution)/shard_map/ppermute | solution.py:118
  138.3 69.9 %copy-start.38 = (f32[8,2]{1,0:T(8,128)}, f32[8,2]{1,0:T(8,128)S(1)}, u32[]{:S(2)}) copy-start(f32[8,2]{1,0:T(8,128)S(1)} %max.41) | copy-start | bytes 196
  161.2 47.8 %copy-start.24 = (pred[128,256]{0,1:T(8,128)(4,1)}, pred[128,256]{0,1:T(8,128)(4,1)S(1)}, u32[]{:S(2)}) copy-start(pred[128,256]{0,1:T(8,128)(4,1)S(1)} %compare_and_fusion) | copy-start | bytes 98308
  222.3 42.1 %copy-start.34 = (f32[3840]{0:T(1024)S(1)}, f32[3840]{0:T(1024)}, u32[]{:S(2)}) copy-start(f32[3840]{0:T(1024)} %get-tuple-element.12) | copy-start | bytes 46084
  222.4 42.1 %copy-start.43 = (f32[1,8192]{1,0:T(1,128)S(1)}, f32[1,8192]{1,0:T(1,128)}, u32[]{:S(2)}) copy-start(f32[1,8192]{1,0:T(1,128)} %get-tuple-element.49) | copy-start | bytes 98308
  263.8 75.0 %copy-start.5 = (bf16[8,128,3840]{2,1,0:T(8,128)(2,1)}, bf16[8,128,3840]{2,1,0:T(8,128)(2,1)S(1)}, u32[]{:S(2)}) copy-start(bf16[8,128,3840]{2,1,0:T(8,128)(2,1)S(1)} %get-tuple-element.61) | copy-start | bytes 23592964
  264.5 74.4 %copy-start.49 = (f32[8,128]{1,0:T(8,128)}, f32[8,128]{1,0:T(8,128)S(1)}, u32[]{:S(2)}) copy-start(f32[8,128]{1,0:T(8,128)S(1)} %get-tuple-element.54) | copy-start | bytes 12292
  404.2 971.0 %reduce-scatter.2.cloned.1.call-start = ((), (), s32[]{:S(2)}) async-start(), calls=%async_computation.2 | async-start | bytes 75497472 | tf_op jit(solution)/shard_map/reduce_scatter | solution.py:137
  404.4 394.1 %copy-start.40 = (f32[8,2]{1,0:T(8,128)}, f32[8,2]{1,0:T(8,128)S(1)}, u32[]{:S(2)}) copy-start(f32[8,2]{1,0:T(8,128)S(1)} %max.44) | copy-start | bytes 196
  884.2 43.3 %copy-start.28 = (f32[8,8,2,128]{3,2,1,0:T(2,128)}, f32[8,8,2,128]{3,2,1,0:T(2,128)S(1)}, u32[]{:S(2)}) copy-start(f32[8,8,2,128]{3,2,1,0:T(2,128)S(1)} %get-tuple-element.64) | copy-start | bytes 196612
  1432.2 85.4 %copy-start.48 = (f32[8,128]{1,0:T(8,128)S(1)}, f32[8,128]{1,0:T(8,128)}, u32[]{:S(2)}) copy-start(f32[8,128]{1,0:T(8,128)} %get-tuple-element.53) | copy-start | bytes 12292
  1652.9 120.3 %collective-permute-start.1 = (bf16[8,128,16,256]{3,1,2,0:T(8,128)(2,1)}, bf16[8,128,16,256]{3,1,2,0:T(8,128)(2,1)}, u32[]{:S(2)}, u32[]{:S(2)}) collective-permute-start(bf16[8,128,16,256]{3,1,2,0:T(8,128)(2,1)} %fusion.55), channel_id=1, source_target_pairs={{1,0},{2,1},{3,2},{4,3},{5,4},{6,5},{7,6}} | collective-permute-start | bytes 25165832 | tf_op jit(solution)/shard_map/ppermute | solution.py:145
  1658.9 41.9 %copy-start.21 = (f32[8,8,2,128]{3,2,1,0:T(2,128)S(1)}, f32[8,8,2,128]{3,2,1,0:T(2,128)}, u32[]{:S(2)}) copy-start(f32[8,8,2,128]{3,2,1,0:T(2,128)} %copy-done.20) | copy-start | bytes 196612
  1658.9 41.9 %copy-start.23 = (f32[8,8,2,128]{3,2,1,0:T(2,128)S(1)}, f32[8,8,2,128]{3,2,1,0:T(2,128)}, u32[]{:S(2)}) copy-start(f32[8,8,2,128]{3,2,1,0:T(2,128)} %copy-done.22) | copy-start | bytes 196612
  1658.9 41.9 %copy-start.29 = (f32[8,8,2,128]{3,2,1,0:T(2,128)S(1)}, f32[8,8,2,128]{3,2,1,0:T(2,128)}, u32[]{:S(2)}) copy-start(f32[8,8,2,128]{3,2,1,0:T(2,128)} %copy-done.28) | copy-start | bytes 196612
  1658.9 41.9 %copy-start.41 = (f32[8,2]{1,0:T(8,128)S(1)}, f32[8,2]{1,0:T(8,128)}, u32[]{:S(2)}) copy-start(f32[8,2]{1,0:T(8,128)} %copy-done.40) | copy-start | bytes 196
  1658.9 42.2 %copy-start.51 = (f32[3840]{0:T(1024)S(1)}, f32[3840]{0:T(1024)}, u32[]{:S(2)}) copy-start(f32[3840]{0:T(1024)} %get-tuple-element.8) | copy-start | bytes 46084
  1659.0 42.8 %copy-start.33 = (f32[3840]{0:T(1024)S(1)}, f32[3840]{0:T(1024)}, u32[]{:S(2)}) copy-start(f32[3840]{0:T(1024)} %get-tuple-element.16) | copy-start | bytes 46084
  1659.0 42.8 %copy-start.32 = (f32[3840]{0:T(1024)S(1)}, f32[3840]{0:T(1024)}, u32[]{:S(2)}) copy-start(f32[3840]{0:T(1024)} %get-tuple-element.48) | copy-start | bytes 46084
  1659.0 42.9 %copy-start.17 = (f32[8,8,2,128]{3,2,1,0:T(2,128)S(1)}, f32[8,8,2,128]{3,2,1,0:T(2,128)}, u32[]{:S(2)}) copy-start(f32[8,8,2,128]{3,2,1,0:T(2,128)} %copy-done.16) | copy-start | bytes 196612
  1659.0 42.9 %copy-start.19 = (f32[8,8,2,128]{3,2,1,0:T(2,128)S(1)}, f32[8,8,2,128]{3,2,1,0:T(2,128)}, u32[]{:S(2)}) copy-start(f32[8,8,2,128]{3,2,1,0:T(2,128)} %copy-done.18) | copy-start | bytes 196612
  1659.0 42.9 %copy-start.39 = (f32[8,2]{1,0:T(8,128)S(1)}, f32[8,2]{1,0:T(8,128)}, u32[]{:S(2)}) copy-start(f32[8,2]{1,0:T(8,128)} %copy-done.38) | copy-start | bytes 196
  1659.0 43.2 %copy-start.3 = (bf16[8,128,8,128]{3,1,2,0:T(8,128)(2,1)S(1)}, bf16[8,128,8,128]{3,1,2,0:T(8,128)(2,1)}, u32[]{:S(2)}) copy-start(bf16[8,128,8,128]{3,1,2,0:T(8,128)(2,1)} %copy-done.2) | copy-start | bytes 6291460
  1854.6 84.7 %copy-start.42 = (f32[1,3840]{1,0:T(1,128)S(1)}, f32[1,3840]{1,0:T(1,128)}, u32[]{:S(2)}) copy-start(f32[1,3840]{1,0:T(1,128)} %stack.33) | copy-start | bytes 46084
  1854.6 85.3 %copy-start.30 = (f32[8192]{0:T(1024)S(1)}, f32[8192]{0:T(1024)}, u32[]{:S(2)}) copy-start(f32[8192]{0:T(1024)} %fusion.39) | copy-start | bytes 98308
  1854.6 85.3 %copy-start.31 = (f32[8192]{0:T(1024)S(1)}, f32[8192]{0:T(1024)}, u32[]{:S(2)}) copy-start(f32[8192]{0:T(1024)} %fusion.37) | copy-start | bytes 98308
  1854.6 86.0 %copy-start.45 = (f32[8,128]{1,0:T(8,128)S(1)}, f32[8,128]{1,0:T(8,128)}, u32[]{:S(2)}) copy-start(f32[8,128]{1,0:T(8,128)} %get-tuple-element.51) | copy-start | bytes 12292
  (30 other events, 472.7 us)
Sparse Core Ops, SparseCore 0:
  404.3 335.9 all-gather.1
  1001.1 374.0 reduce-scatter.1
where the time goes:
time: 1970 us; the launch traced here: 1960 us
  matrix products  784 us (40%)
  waiting for transfers between devices  472 us (24%)
  local copies, waits for them, and re-layouts  362 us (18%)
  other arithmetic  320 us (16%)
    reduce_scatter x1, waiting for transfers between devices, local_step(): lax.psum_scatter(jnp.concatenate([dk_far, dv_far], axis=2).astype(jnp.bfl...  256 us
    all_gather x1, waiting for transfers between devices, local_step(): lax.all_gather(jnp.concatenate([keys_two, values_two], axis=2), 'cp', axi...  216 us
    dot_general x2, matrix products, project_backward(): jnp.einsum('bsq,dq->bsd', d_proj.astype(jnp.bfloat16), w_in, preferred_el...  170 us
    dot_general x2, matrix products, norm_project(): jnp.dot(normed, w_in, preferred_element_type=jnp.float32) + bias_row  149 us
    dot_general x2, matrix products, dense_out(): jnp.dot(attn_out.reshape(batch_size, seq_dev, -1), w_proj, preferred_elem...  83.2 us
    dot_general x2, matrix products, attend_backward(): jnp.einsum('bqkgd,bskd->bkgqs', d_attn, value_rows, preferred_element_typ...  64.1 us
    convert_element_type x2, other arithmetic, attend_backward(): d_scores = (prob_f32 * (d_prob - row_delta[..., None])).astype(jnp.bfloat16)  56.8 us
    dot_general x2, matrix products, attend_backward(): jnp.einsum('bkgqs,bqkgd->bskd', prob_bf, d_attn, preferred_element_type=j...  53.4 us
  transfers between devices with their start and end apart: 4, of which 2 were waited for; matrix products, arithmetic and copies ran while one was open for 21% of the time, Pallas kernels for 0%

commit v1 on v0

v1 whole, which is shorter than its diff:
```python
import functools
import jax
import jax.numpy as jnp
import math
from jax import lax
from jax.experimental import pallas as pl
from jax.experimental.pallas import tpu as pltpu
from jax.sharding import PartitionSpec as P

EPSILON = 1e-5
ROPE_THETA = 150000.0
YARN_FACTOR = 32.0
YARN_CONTEXT = 4096.0
YARN_ALPHA = 1.0
YARN_BETA = 32.0
LOG2E = 1.4426950408889634
VMEM_LIMIT = 66_000_000
BF = jnp.bfloat16
F32 = jnp.float32


def rope_tables(positions, head_dim):
    half_dim = head_dim // 2
    freq_steps = jnp.arange(half_dim, dtype=jnp.float32)
    freq_base = ROPE_THETA ** (freq_steps * 2.0 / head_dim)
    concentration = 0.1 * math.log(YARN_FACTOR) + 1.0
    low_edge = half_dim * math.log(YARN_CONTEXT / (YARN_BETA * 2.0 * math.pi)) / math.log(ROPE_THETA)
    high_edge = half_dim * math.log(YARN_CONTEXT / (YARN_ALPHA * 2.0 * math.pi)) / math.log(ROPE_THETA)
    ramp_pos = jnp.clip((freq_steps - low_edge) / (high_edge - low_edge), 0.0, 1.0)
    inv_freq = (1.0 - ramp_pos) / freq_base + ramp_pos / (YARN_FACTOR * freq_base)
    angles = positions.astype(jnp.float32)[:, None] * inv_freq[None, :]
    return jnp.cos(angles) * concentration, jnp.sin(angles) * concentration


def dot_nn(a, b):
    return lax.dot_general(a, b, (((1,), (0,)), ((), ())), preferred_element_type=F32)


def dot_nt(a, b):
    return lax.dot_general(a, b, (((1,), (1,)), ((), ())), preferred_element_type=F32)


def dot_tn(a, b):
    return lax.dot_general(a, b, (((0,), (0,)), ((), ())), preferred_element_type=F32)


def rotate(block, cos, sin):
    half = block.shape[1] // 2
    lo, hi = block[:, :half], block[:, half:]
    return jnp.concatenate([lo * cos - hi * sin, hi * cos + lo * sin], axis=1)


def window_mask(keys, cols):
    key = lax.broadcasted_iota(jnp.int32, (keys, cols), 0) + (256 - keys)
    row = lax.rem(lax.broadcasted_iota(jnp.int32, (keys, cols), 1), 128)
    return (key >= row) & (key <= row + 128)


def causal_mask(size, cols):
    key = lax.broadcasted_iota(jnp.int32, (size, cols), 0)
    row = lax.rem(lax.broadcasted_iota(jnp.int32, (size, cols), 1), size)
    return key <= row


def spans(window_on, rows):
    if window_on:
        return [(r, 128, max(r - 128, 0), r + 128, min(256, r + 128)) for r in range(0, rows, 128)][::-1]
    return [(r, 256, 0, r + 256, 256) for r in range(0, rows, 256)][::-1]


def masked_logits(s, mask, count):
    if count == s.shape[0]:
        return jnp.where(mask, s, -jnp.inf)
    return jnp.concatenate([s[:-count], jnp.where(mask, s[-count:], -jnp.inf)], axis=0)


def forward_kernel(layer, window_on, scale, x_ref, gain_ref, wq_ref, wk_ref, wv_ref, bq_ref, bk_ref, bv_ref, cos_ref, sin_ref, sink_ref, q_ref, k_ref, v_ref, o_ref, lse_ref, n_ref):
    head = pl.program_id(0)
    rows = x_ref.shape[0]
    hd = k_ref.shape[1]

    @pl.when(head == 0)
    def _():
        def norm(i, c):
            part = pl.ds(pl.multiple_of(i * 64, 64), 64)
            f = x_ref[part, :].astype(F32)
            inv = lax.rsqrt(jnp.mean(f * f, axis=1, keepdims=True) + EPSILON)
            n_ref[part, :] = (f * inv * gain_ref[...]).astype(BF)
            return c

        lax.fori_loop(0, rows // 64, norm, 0)

    step = min(512, rows)
    for r in range(0, rows, step):
        part = slice(r, r + step)
        n = n_ref[part, :]
        cos, sin = cos_ref[part, :], sin_ref[part, :]
        tq = dot_nn(n, wq_ref[...]) + bq_ref[...]
        q_ref[part, :hd] = rotate(tq[:, :hd], cos, sin).astype(BF)
        q_ref[part, hd:] = rotate(tq[:, hd:], cos, sin).astype(BF)
        k_ref[part, :] = rotate(dot_nn(n, wk_ref[...]) + bk_ref[...], cos, sin).astype(BF)
        v_ref[part, :] = (dot_nn(n, wv_ref[...]) + bv_ref[...]).astype(BF)

    factor = scale * LOG2E
    sink0 = sink_ref[layer, 2 * head] * LOG2E
    sink1 = sink_ref[layer, 2 * head + 1] * LOG2E
    for r, size, k0, k1, masked in spans(window_on, rows):
        part = slice(r, r + size)
        q2 = jnp.concatenate([q_ref[part, :hd], q_ref[part, hd:]], axis=0)
        mask = window_mask(masked, 2 * size) if window_on else causal_mask(masked, 2 * size)
        s = masked_logits(dot_nt(k_ref[k0:k1, :], q2) * factor, mask, masked)
        sink = jnp.where(lax.broadcasted_iota(jnp.int32, (1, 2 * size), 1) < size, sink0, sink1)
        peak = jnp.maximum(jnp.max(s, axis=0, keepdims=True), sink)
        e = jnp.exp2(s - peak)
        denom = jnp.sum(e, axis=0, keepdims=True) + jnp.exp2(sink - peak)
        p = (e * (1.0 / denom)).astype(BF)
        o = dot_tn(p, v_ref[k0:k1, :]).astype(BF)
        o_ref[part, :hd] = o[:size]
        o_ref[part, hd:] = o[size:]
        lse = peak + jnp.log(denom) * LOG2E
        lse_ref[0:1, part] = lse[:, :size]
        lse_ref[1:2, part] = lse[:, size:]


def forward_attention(layer, window_on, x, gain, w_qkv, b_qkv, cos, sin, sinks, heads, kv):
    rows, d = x.shape
    hd = w_qkv.shape[2] // (heads + 2 * kv)
    half = hd // 2
    once = pl.Buffered(1)
    whole = lambda h: (0, 0)
    in_specs = [
        pl.BlockSpec((rows, d), whole, pipeline_mode=once),
        pl.BlockSpec((None, 1, d), lambda h: (layer, 0, 0)),
        pl.BlockSpec((None, d, 2 * hd), lambda h: (layer, 0, h)),
        pl.BlockSpec((None, d, hd), lambda h: (layer, 0, heads + h)),
        pl.BlockSpec((None, d, hd), lambda h: (layer, 0, heads + kv + h)),
        pl.BlockSpec((None, 1, 2 * hd), lambda h: (layer, 0, h)),
        pl.BlockSpec((None, 1, hd), lambda h: (layer, 0, heads + h)),
        pl.BlockSpec((None, 1, hd), lambda h: (layer, 0, heads + kv + h)),
        pl.BlockSpec((rows, half), whole, pipeline_mode=once),
        pl.BlockSpec((rows, half), whole, pipeline_mode=once),
        pl.BlockSpec(memory_space=pltpu.SMEM),
    ]
    out_specs = [
        pl.BlockSpec((rows, 2 * hd), lambda h: (0, h)),
        pl.BlockSpec((rows, hd), lambda h: (0, h)),
        pl.BlockSpec((rows, hd), lambda h: (0, h)),
        pl.BlockSpec((rows, 2 * hd), lambda h: (0, h)),
        pl.BlockSpec((None, 2, rows), lambda h: (h, 0, 0)),
    ]
    out_shape = [
        jax.ShapeDtypeStruct((rows, heads * hd), BF),
        jax.ShapeDtypeStruct((rows, kv * hd), BF),
        jax.ShapeDtypeStruct((rows, kv * hd), BF),
        jax.ShapeDtypeStruct((rows, heads * hd), BF),
        jax.ShapeDtypeStruct((kv, 2, rows), F32),
    ]
    return pl.pallas_call(
        functools.partial(forward_kernel, layer, window_on, hd ** -0.5),
        grid=(kv,), in_specs=in_specs, out_specs=out_specs, out_shape=out_shape,
        scratch_shapes=[pltpu.VMEM((rows, d), BF)],
        compiler_params=pltpu.CompilerParams(dimension_semantics=("arbitrary",), vmem_limit_bytes=VMEM_LIMIT),
        cost_estimate=pl.CostEstimate(flops=2 * rows * d * w_qkv.shape[2] + 8 * rows * rows * heads * hd // 4, bytes_accessed=2 * d * w_qkv.shape[2], transcendentals=0),
    )(x, gain, w_qkv, w_qkv, w_qkv, b_qkv, b_qkv, b_qkv, cos, sin, sinks)


def backward_kernel(layer, window_on, scale, dy_ref, wo_ref, q_ref, k_ref, v_ref, lse_ref, cos_ref, sin_ref, sink_ref, dp_ref, db_ref, ds_ref, do_ref, dk_ref, dv_ref):
    head = pl.program_id(0)
    rows = dy_ref.shape[0]
    hd = k_ref.shape[1]
    chunk = rows // db_ref.shape[0]
    step = min(512, rows)
    for r in range(0, rows, step):
        do_ref[r:r + step, :] = dot_nt(dy_ref[r:r + step, :], wo_ref[...]).astype(BF)

    factor = scale * LOG2E
    sink0 = sink_ref[layer, 2 * head] * LOG2E
    sink1 = sink_ref[layer, 2 * head + 1] * LOG2E

    def finish(block, part, col, turn):
        f = block.astype(BF).astype(F32)
        if turn:
            f = rotate(f, cos_ref[part, :], -sin_ref[part, :])
        dp_ref[part, col:col + hd] = f.astype(BF)
        for i in range(0, f.shape[0], chunk):
            c = (part.start + i) // chunk
            db_ref[c:c + 1, col:col + hd] = jnp.sum(f[i:i + chunk], axis=0, keepdims=True)

    for r, size, k0, k1, masked in spans(window_on, rows):
        part = slice(r, r + size)
        q2 = jnp.concatenate([q_ref[part, :hd], q_ref[part, hd:]], axis=0)
        do2 = jnp.concatenate([do_ref[part, :hd], do_ref[part, hd:]], axis=0)
        lse = jnp.concatenate([lse_ref[0:1, part], lse_ref[1:2, part]], axis=1)
        keys, values = k_ref[k0:k1, :], v_ref[k0:k1, :]
        mask = window_mask(masked, 2 * size) if window_on else causal_mask(masked, 2 * size)
        s = masked_logits(dot_nt(keys, q2) * factor, mask, masked)
        p = jnp.exp2(s - lse)
        g = dot_nt(values, do2).astype(BF).astype(F32)
        delta = jnp.sum(p * g, axis=0, keepdims=True)
        ds = (p * (g - delta)).astype(BF)
        sink = jnp.where(lax.broadcasted_iota(jnp.int32, (1, 2 * size), 1) < size, sink0, sink1)
        sd = jnp.exp2(sink - lse) * delta
        ds_ref[0:1, part] = sd[:, :size]
        ds_ref[1:2, part] = sd[:, size:]
        dv = dot_nn(p.astype(BF), do2)
        dk = dot_nn(ds, q2)
        fresh = r + size == rows
        if fresh:
            dv_ref[k0:k1, :] = dv
            dk_ref[k0:k1, :] = dk
        elif window_on:
            own = k1 - size
            dv_ref[own:k1, :] += dv[own - k0:]
            dk_ref[own:k1, :] += dk[own - k0:]
            if own > k0:
                dv_ref[k0:own, :] = dv[:own - k0]
                dk_ref[k0:own, :] = dk[:own - k0]
        else:
            dv_ref[k0:k1, :] += dv
            dk_ref[k0:k1, :] += dk
        dq = dot_tn(ds, keys) * scale
        finish(dq[:size], part, 0, True)
        finish(dq[size:], part, hd, True)
        finish(dk_ref[part, :] * scale, part, 2 * hd, True)
        finish(dv_ref[part, :], part, 3 * hd, False)


def backward_attention(layer, window_on, dy, w_out, q, k, v, lse, cos, sin, sinks, chunks):
    rows, d = dy.shape
    kv = lse.shape[0]
    hd = k.shape[1] // kv
    half = hd // 2
    once = pl.Buffered(1)
    whole = lambda h: (0, 0)
    in_specs = [
        pl.BlockSpec((rows, d), whole, pipeline_mode=once),
        pl.BlockSpec((None, 2 * hd, d), lambda h: (layer, h, 0)),
        pl.BlockSpec((rows, 2 * hd), lambda h: (0, h)),
        pl.BlockSpec((rows, hd), lambda h: (0, h)),
        pl.BlockSpec((rows, hd), lambda h: (0, h)),
        pl.BlockSpec((None, 2, rows), lambda h: (h, 0, 0)),
        pl.BlockSpec((rows, half), whole, pipeline_mode=once),
        pl.BlockSpec((rows, half), whole, pipeline_mode=once),
        pl.BlockSpec(memory_space=pltpu.SMEM),
    ]
    out_specs = [
        pl.BlockSpec((None, rows, 4 * hd), lambda h: (h, 0, 0)),
        pl.BlockSpec((chunks, 4 * hd), lambda h: (0, h)),
        pl.BlockSpec((None, 2, rows), lambda h: (h, 0, 0)),
    ]
    out_shape = [
        jax.ShapeDtypeStruct((kv, rows, 4 * hd), BF),
        jax.ShapeDtypeStruct((chunks, kv * 4 * hd), F32),
        jax.ShapeDtypeStruct((kv, 2, rows), F32),
    ]
    return pl.pallas_call(
        functools.partial(backward_kernel, layer, window_on, hd ** -0.5),
        grid=(kv,), in_specs=in_specs, out_specs=out_specs, out_shape=out_shape,
        scratch_shapes=[pltpu.VMEM((rows, 2 * hd), BF), pltpu.VMEM((rows, hd), F32), pltpu.VMEM((rows, hd), F32)],
        compiler_params=pltpu.CompilerParams(dimension_semantics=("arbitrary",), vmem_limit_bytes=VMEM_LIMIT),
        cost_estimate=pl.CostEstimate(flops=2 * rows * d * 2 * kv * hd + 20 * rows * rows * 2 * kv * hd // 4, bytes_accessed=2 * d * 2 * kv * hd, transcendentals=0),
    )(dy, w_out, q, k, v, lse, cos, sin, sinks)


def input_kernel(chunk, dp_ref, wq_ref, wk_ref, wv_ref, x_ref, gain_ref, res_ref, out_ref, dg_ref, db_ref, acc_ref):
    step = pl.program_id(1)
    rows, d = acc_ref.shape
    tile = 768
    dp = dp_ref[...]

    def product(n):
        part = slice(n, n + tile)
        return dot_nt(dp, jnp.concatenate([wq_ref[part, :], wk_ref[part, :], wv_ref[part, :]], axis=1))

    @pl.when(step == 0)
    def _():
        for n in range(0, d, tile):
            acc_ref[:, n:n + tile] = product(n)

    @pl.when(step > 0)
    def _():
        for n in range(0, d, tile):
            acc_ref[:, n:n + tile] += product(n)

    @pl.when(step == pl.num_programs(1) - 1)
    def _():
        sub = 32
        gain = gain_ref[...]

        def finish(i, c):
            def piece(j, carry):
                dg, db = carry
                part = pl.ds(pl.multiple_of(i * chunk + j * sub, sub), sub)
                dn = acc_ref[part, :].astype(BF).astype(F32)
                f = x_ref[part, :].astype(F32)
                inv = lax.rsqrt(jnp.mean(f * f, axis=1, keepdims=True) + EPSILON)
                unit = dn * gain
                dot = jnp.mean(unit * f, axis=1, keepdims=True)
                dh = inv * unit - f * (inv * inv * inv * dot)
                out = (res_ref[part, :].astype(F32) + dh).astype(BF)
                out_ref[part, :] = out
                dg = dg + jnp.sum(dn * f * inv, axis=0, keepdims=True)
                db = db + jnp.sum(out.astype(F32), axis=0, keepdims=True)
                return dg, db

            zero = jnp.zeros((1, d), F32)
            dg, db = lax.fori_loop(0, chunk // sub, piece, (zero, zero))
            dg_ref[i] = dg
            db_ref[i] = db
            return c

        lax.fori_loop(0, rows // chunk, finish, 0)


def input_gradient(layer, dproj, w_qkv, x, gain, residual, heads, chunks):
    kv, rows, width = dproj.shape
    d = x.shape[1]
    hd = width // 4
    parts = 2
    m = rows // parts
    chunk = rows // chunks
    once = pl.Buffered(1)
    row = lambda i, h: (i, 0)
    in_specs = [
        pl.BlockSpec((None, m, width), lambda i, h: (h, i, 0)),
        pl.BlockSpec((None, d, 2 * hd), lambda i, h: (layer, 0, h)),
        pl.BlockSpec((None, d, hd), lambda i, h: (layer, 0, heads + h)),
        pl.BlockSpec((None, d, hd), lambda i, h: (layer, 0, heads + kv + h)),
        pl.BlockSpec((m, d), row),
        pl.BlockSpec((None, 1, d), lambda i, h: (layer, 0, 0)),
        pl.BlockSpec((m, d), row),
    ]
    out_specs = [
        pl.BlockSpec((m, d), row),
        pl.BlockSpec((m // chunk, 1, d), lambda i, h: (i, 0, 0)),
        pl.BlockSpec((m // chunk, 1, d), lambda i, h: (i, 0, 0)),
    ]
    out_shape = [
        jax.ShapeDtypeStruct((rows, d), BF),
        jax.ShapeDtypeStruct((chunks, 1, d), F32),
        jax.ShapeDtypeStruct((chunks, 1, d), F32),
    ]
    return pl.pallas_call(
        functools.partial(input_kernel, chunk),
        grid=(parts, kv), in_specs=in_specs, out_specs=out_specs, out_shape=out_shape,
        scratch_shapes=[pltpu.VMEM((m, d), F32)],
        compiler_params=pltpu.CompilerParams(dimension_semantics=("arbitrary", "arbitrary"), vmem_limit_bytes=VMEM_LIMIT),
        cost_estimate=pl.CostEstimate(flops=2 * rows * d * w_qkv.shape[2], bytes_accessed=4 * d * w_qkv.shape[2], transcendentals=0),
    )(dproj, w_qkv, w_qkv, w_qkv, x, gain, residual)


def solution(mesh):
    chunks = mesh.shape['cp']
    row_spec = P('dp', 'cp')
    device_spec = P(('dp', 'cp'))
    whole_spec = P()

    def step(hidden, grad_out, norm_gain, w_qkv, b_qkv, w_out, b_out, attn_sinks):
        batch, seq_dev, d = hidden.shape
        heads = attn_sinks.shape[1]
        hd = w_out.shape[1] // heads
        kv = (w_qkv.shape[2] // hd - heads) // 2
        rows = chunks * seq_dev
        cos, sin = rope_tables(jnp.arange(rows), hd)
        gain = norm_gain[:, None, :]
        bias = b_qkv[:, None, :]

        def exchange(block):
            return lax.all_to_all(block, 'cp', 0, 0, tiled=True)

        def total(parts):
            return jnp.sum(exchange(jnp.concatenate(parts, axis=1)), axis=0)

        x = exchange(hidden).reshape(rows, d)
        dy = exchange(grad_out).reshape(rows, d)

        def dense(layer, o, h):
            t = jnp.dot(o, w_out[layer], preferred_element_type=F32) + b_out[layer]
            return (h.astype(F32) + t).astype(BF)

        q1, k1, v1, o1, lse1 = forward_attention(0, True, x, gain, w_qkv, bias, cos, sin, attn_sinks, heads, kv)
        mid = dense(0, o1, x)
        q2, k2, v2, o2, lse2 = forward_attention(1, False, mid, gain, w_qkv, bias, cos, sin, attn_sinks, heads, kv)
        out_rows, dy = lax.optimization_barrier((dense(1, o2, mid), dy))
        output = exchange(out_rows.reshape(batch, seq_dev, d))

        def sink_rows(s):
            return -jnp.sum(s.reshape(heads, chunks, seq_dev), axis=2).T

        dproj2, dbias2, dsink2 = backward_attention(1, False, dy, w_out, q2, k2, v2, lse2, cos, sin, attn_sinks, chunks)
        d_mid, dgain2, dbout1 = input_gradient(1, dproj2, w_qkv, mid, gain, dy, heads, chunks)
        d_mid, output = lax.optimization_barrier((d_mid, output))
        dproj1, dbias1, dsink1 = backward_attention(0, True, d_mid, w_out, q1, k1, v1, lse1, cos, sin, attn_sinks, chunks)
        early = total([dbias2, dgain2[:, 0], dbout1[:, 0], sink_rows(dsink2)])
        dproj1, early = lax.optimization_barrier((dproj1, early))
        d_x, dgain1, _ = input_gradient(0, dproj1, w_qkv, x, gain, d_mid, heads, chunks)
        d_hidden = exchange(d_x.reshape(batch, seq_dev, d))

        wide = kv * 4 * hd
        late = total([dbias1, dgain1[:, 0], sink_rows(dsink1)])

        def split_bias(b):
            b = b.reshape(kv, 4 * hd)
            return jnp.concatenate([b[:, :2 * hd].reshape(-1), b[:, 2 * hd:3 * hd].reshape(-1), b[:, 3 * hd:].reshape(-1)])

        d_gain = jnp.stack([late[wide:wide + d], early[wide:wide + d]])[None]
        d_bias_qkv = jnp.stack([split_bias(late[:wide]), split_bias(early[:wide])])[None]
        d_bias_out = jnp.stack([early[wide + d:wide + 2 * d], jnp.sum(grad_out.astype(F32), axis=(0, 1))])[None]
        d_sinks = jnp.stack([late[wide + d:], early[wide + 2 * d:]])[None]
        return output, d_hidden, d_gain, d_bias_qkv, d_bias_out, d_sinks

    return jax.shard_map(step, mesh=mesh, in_specs=(row_spec, row_spec, whole_spec, whole_spec, whole_spec, whole_spec, whole_spec, whole_spec), out_specs=(row_spec, row_spec, device_spec, device_spec, device_spec, device_spec), check_vma=False)
```

time: 1970 us -> 928 us (0.47)
  matrix products: 784 us -> 80.6 us
  Pallas kernels: 0 us -> 517 us
  local copies, waits for them, and re-layouts: 362 us -> 19.2 us
  other arithmetic: 320 us -> 11.6 us
  waiting for transfers between devices: 472 us -> 243 us
    dot_general x20 -> x2, matrix products: 784 us -> 80.6 us  [dense(): t = jnp.dot(o, w_out[layer], preferred_element_type=F32) + b_out[layer]]
    pallas_call x0 -> x6, Pallas kernels: none -> 517 us  [the longest x2 195 us: input_gradient(): pl.pallas_call(functools.partial(input_kernel, chunk), grid=(parts, kv),...]
    reduce_scatter x1 -> x0, waiting for transfers between devices: 256 us -> none  [local_step(): lax.psum_scatter(jnp.concatenate([dk_far, dv_far], axis=2).astype(jnp.bfl...]
    all_to_all x0 -> x4, waiting for transfers between devices: none -> 243 us  [exchange(): return lax.all_to_all(block, 'cp', 0, 0, tiled=True)]
    all_gather x1 -> x0, waiting for transfers between devices: 216 us -> none  [local_step(): lax.all_gather(jnp.concatenate([keys_two, values_two], axis=2), 'cp', axi...]
    reshape x11 -> x4, local copies, waits for them, and re-layouts: 136 us -> 0.14 us  [the longest x2 0.11 us: sink_rows(): return -jnp.sum(s.reshape(heads, chunks, seq_dev), axis=2).T]
    slice x18 -> x6, local copies, waits for them, and re-layouts: 126 us -> 0.67 us  [the longest x1 0.65 us: dense(): t = jnp.dot(o, w_out[layer], preferred_element_type=F32) + b_out[layer]]
    convert_element_type x6 -> x0, other arithmetic: 105 us -> none  [the longest x2 56.8 us: attend_backward(): d_scores = (prob_f32 * (d_prob - row_delta[..., None])).astype(jnp.bfloat16)]
  transfers between devices with their start and end apart: 4 -> 4, of which waited for: 2 -> 3; matrix products, arithmetic and copies ran while one was open for 21% -> 10% of each run, Pallas kernels for 0% -> 20%
where the time goes in v1:
time: 928 us; the launch traced here: 916 us
  Pallas kernels  517 us (56%)
  waiting for transfers between devices  243 us (26%)
  matrix products  80.6 us (9%)
  starting transfers between devices  23.1 us (2%)
  local copies, waits for them, and re-layouts  19.2 us (2%)
  blocking collectives  19.1 us (2%)
  other arithmetic  11.6 us (1%)
    all_to_all x4, waiting for transfers between devices, exchange(): return lax.all_to_all(block, 'cp', 0, 0, tiled=True)  243 us
    pallas_call x2, Pallas kernels, input_gradient(): pl.pallas_call(functools.partial(input_kernel, chunk), grid=(parts, kv),...  195 us
    pallas_call x2, Pallas kernels, forward_attention(): pl.pallas_call(functools.partial(forward_kernel, layer, window_on, hd **...  183 us
    pallas_call x2, Pallas kernels, backward_attention(): pl.pallas_call(functools.partial(backward_kernel, layer, window_on, hd **...  139 us
    dot_general x2, matrix products, dense(): t = jnp.dot(o, w_out[layer], preferred_element_type=F32) + b_out[layer]  80.6 us
    all_to_all x4, starting transfers between devices, exchange(): return lax.all_to_all(block, 'cp', 0, 0, tiled=True)  23.1 us
    all_to_all x2, blocking collectives, exchange(): return lax.all_to_all(block, 'cp', 0, 0, tiled=True)  19.1 us
  transfers between devices with their start and end apart: 4, of which 3 were waited for; matrix products, arithmetic and copies ran while one was open for 10% of the time, Pallas kernels for 20%

profile of v1, /device:TPU:7, one launch (start us, length us, event | category | flops | bytes accessed | tf_op | source)
XLA Modules:
  0.0 915.5 jit_solution(15367476046599246320)
XLA Ops:
  0.7 3.7 all-to-all-start
  4.4 0.6 broadcast_in_dim.20.gain_ref
  5.0 0.7 broadcast_in_dim.21.bq_ref.bk_ref.bv_ref
  5.7 0.7 slice_reduce_fusion
  6.4 3.1 fusion.11
  9.5 80.3 %all-to-all-done = bf16[8,128,3840]{2,1,0:T(8,128)(2,1)} async-done(((bf16[8,128,3840]{2,1,0:T(8,128)(2,1)}), bf16[8,128,3840]{2,1,0:T(8,128)(2,1)}, u32[]{:S(2)}, u32[]{:S(2)}) %all-to-all-start) | async-done | bytes 7864352 | tf_op jit(solution)/shard_map/all_to_all | solution.py:369
  89.7 6.7 all-to-all-start.1
  96.4 86.8 %shard_map.127 = (bf16[1024,4096]{1,0:T(8,128)(2,1)}, bf16[1024,2048]{1,0:T(8,128)(2,1)}, bf16[1024,2048]{1,0:T(8,128)(2,1)}, bf16[1024,4096]{1,0:T(8,128)(2,1)}, f32[8,2,1024]{2,1,0:T(2,128)}) custom-call(bf16[1024,3840]{1,0:T(8,128)(2,1)} %bitcast.x_ref, f32[2,1,3840]{2,1,0:T(1,128)} %broadcast_in_dim.20.gain_ref, bf16[2,3840,8192]{2,1,0:T(8,128)(2,1)} %wv_ref.7, ...), custom_call_target="tpu_custom_call" | custom-call | flops 73014444032 | bytes 62914560 | tf_op jit(solution)/shard_map/pallas_call | solution.py:158
  183.2 40.2 %add_convert_fusion.1.x_ref = bf16[1024,3840]{1,0:T(8,128)(2,1)} fusion(bf16[1024,3840]{1,0:T(8,128)(2,1)} %bitcast.x_ref, f32[3840]{0:T(1024)S(1)} %get-tuple-element.61, bf16[1024,4096]{1,0:T(8,128)(2,1)} %get-tuple-element.33, bf16[2,4096,3840]{2,1,0:T(8,128)(2,1)} %wo_ref.3), kind=kOutput, calls=%fused_computation.8 | convolution fusion | flops 32227983360 | bytes 55589888 | tf_op jit(solution)/shard_map/dot_general | solution.py:378
  223.5 96.6 %shard_map.128 = (bf16[1024,4096]{1,0:T(8,128)(2,1)}, bf16[1024,2048]{1,0:T(8,128)(2,1)}, bf16[1024,2048]{1,0:T(8,128)(2,1)}, bf16[1024,4096]{1,0:T(8,128)(2,1)}, f32[8,2,1024]{2,1,0:T(2,128)}) custom-call(bf16[1024,3840]{1,0:T(8,128)(2,1)} %add_convert_fusion.1.x_ref, f32[2,1,3840]{2,1,0:T(1,128)} %broadcast_in_dim.20.gain_ref, ...), custom_call_target="tpu_custom_call" | custom-call | flops 73014444032 | bytes 62914560 | tf_op jit(solution)/shard_map/pallas_call | solution.py:158
  320.1 40.4 %add_convert_fusion = bf16[1024,3840]{1,0:T(8,128)(2,1)} fusion(bf16[1024,3840]{1,0:T(8,128)(2,1)} %add_convert_fusion.1.x_ref, f32[3840]{0:T(1024)S(1)} %copy-done.8, bf16[1024,4096]{1,0:T(8,128)(2,1)} %get-tuple-element.34, bf16[2,4096,3840]{2,1,0:T(8,128)(2,1)} %wo_ref.3), kind=kOutput, calls=%fused_computation.7 | convolution fusion | flops 32227983360 | bytes 55589888 | tf_op jit(solution)/shard_map/dot_general | solution.py:378
  360.5 74.0 %shard_map.129 = (bf16[8,1024,1024]{2,1,0:T(8,128)(2,1)}, f32[8,8192]{1,0:T(8,128)}, f32[8,2,1024]{2,1,0:T(2,128)}) custom-call(bf16[1024,3840]{1,0:T(8,128)(2,1)} %bitcast.3.dy_ref.res_ref, bf16[2,4096,3840]{2,1,0:T(8,128)(2,1)} %wo_ref.3, bf16[1024,4096]{1,0:T(8,128)(2,1)} %get-tuple-element.36.q_ref, bf16[1024,2048]{1,0:T(8,128)(2,1)} %get-tuple-element.37.k_ref, ...), custom_call_target="tpu_custom_call" | custom-call | flops 53687091200 | bytes 31457280 | tf_op jit(solution)/shard_map/pallas_call | solution.py:256
  434.5 97.7 %shard_map.130 = (bf16[1024,3840]{1,0:T(8,128)(2,1)}, f32[8,1,3840]{2,1,0:T(1,128)}, f32[8,1,3840]{2,1,0:T(1,128)}) custom-call(bf16[8,1024,1024]{2,1,0:T(8,128)(2,1)} %get-tuple-element.40.dp_ref, bf16[2,3840,8192]{2,1,0:T(8,128)(2,1)} %wv_ref.7, bf16[2,3840,8192]{2,1,0:T(8,128)(2,1)} %wv_ref.7, bf16[2,3840,8192]{2,1,0:T(8,128)(2,1)} %wv_ref.7, ...), custom_call_target="tpu_custom_call" | custom-call | flops 64424509440 | bytes 125829120 | tf_op jit(solution)/shard_map/pallas_call | solution.py:343
  532.5 1.0 copy_bitcast_fusion.1
  533.5 0.5 copy.15
  534.1 9.7 %all_to_all.38 = f32[8,1,15888]{2,1,0:T(1,128)S(1)} all-to-all(f32[8,1,15888]{2,1,0:T(1,128)S(1)} %copy.15), channel_id=1, replica_groups=mesh['dp'=1,'cp'=8] {'cp'}, dimensions={0} | all-to-all | bytes 1016832 | tf_op jit(solution)/shard_map/all_to_all | solution.py:369
  543.7 6.3 all-to-all-start.2
  550.0 1.1 reduce_sum.46
  551.1 84.8 %all-to-all-done.2 = bf16[8,128,3840]{2,1,0:T(8,128)(2,1)} async-done(((bf16[8,128,3840]{2,1,0:T(8,128)(2,1)}), bf16[8,128,3840]{2,1,0:T(8,128)(2,1)}, u32[]{:S(2)}, u32[]{:S(2)}) %all-to-all-start.2) | async-done | bytes 7864352 | tf_op jit(solution)/shard_map/all_to_all | solution.py:369
  635.9 64.6 %shard_map.131 = (bf16[8,1024,1024]{2,1,0:T(8,128)(2,1)}, f32[8,8192]{1,0:T(8,128)}, f32[8,2,1024]{2,1,0:T(2,128)}) custom-call(bf16[1024,3840]{1,0:T(8,128)(2,1)} %get-tuple-element.44.dy_ref.res_ref, bf16[2,4096,3840]{2,1,0:T(8,128)(2,1)} %wo_ref.3, bf16[1024,4096]{1,0:T(8,128)(2,1)} %get-tuple-element.45.q_ref, ...), custom_call_target="tpu_custom_call" | custom-call | flops 53687091200 | bytes 31457280 | tf_op jit(solution)/shard_map/pallas_call | solution.py:256
  700.5 97.6 %shard_map.132 = (bf16[1024,3840]{1,0:T(8,128)(2,1)}, f32[8,1,3840]{2,1,0:T(1,128)}, f32[8,1,3840]{2,1,0:T(1,128)}) custom-call(bf16[8,1024,1024]{2,1,0:T(8,128)(2,1)} %get-tuple-element.54.dp_ref, bf16[2,3840,8192]{2,1,0:T(8,128)(2,1)} %wv_ref.7, bf16[2,3840,8192]{2,1,0:T(8,128)(2,1)} %wv_ref.7, bf16[2,3840,8192]{2,1,0:T(8,128)(2,1)} %wv_ref.7, ...), custom_call_target="tpu_custom_call" | custom-call | flops 64424509440 | bytes 125829120 | tf_op jit(solution)/shard_map/pallas_call | solution.py:343
  798.1 0.9 copy.30
  799.7 9.4 %all_to_all.39 = f32[8,1,12048]{2,1,0:T(1,128)S(1)} all-to-all(f32[8,1,12048]{2,1,0:T(1,128)S(1)} %copy.17), channel_id=1, replica_groups=mesh['dp'=1,'cp'=8] {'cp'}, dimensions={0} | all-to-all | bytes 771072 | tf_op jit(solution)/shard_map/all_to_all | solution.py:369
  809.1 6.4 all-to-all-start.4
  815.5 4.3 convert_reduce_fusion
  820.0 0.6 maximum_bitcast_fusion.4
  821.1 0.6 maximum_bitcast_fusion.5
  821.7 0.6 maximum_bitcast_fusion.3
  822.3 0.7 maximum_bitcast_fusion.2
  823.0 78.3 %all-to-all-done.4 = bf16[8,128,3840]{2,1,0:T(8,128)(2,1)} async-done(((bf16[8,128,3840]{2,1,0:T(8,128)(2,1)}), bf16[8,128,3840]{2,1,0:T(8,128)(2,1)}, u32[]{:S(2)}, u32[]{:S(2)}) %all-to-all-start.4) | async-done | bytes 7864352 | tf_op jit(solution)/shard_map/all_to_all | solution.py:369
  901.3 7.0 copy.33
  908.3 7.0 copy.34
  (58 shorter events, 1.4 us)
Async XLA Ops:
  0.6 3.7 copy-start.6
  0.6 4.4 copy-start.3
  0.7 5.1 copy-start.7
  0.7 89.1 %all-to-all-start = ((bf16[8,128,3840]{2,1,0:T(8,128)(2,1)}), bf16[8,128,3840]{2,1,0:T(8,128)(2,1)}, u32[]{:S(2)}, u32[]{:S(2)}) async-start(bf16[8,128,3840]{2,1,0:T(8,128)(2,1)} %param.8), calls=%async_computation | async-start | bytes 15728640 | tf_op jit(solution)/shard_map/all_to_all | solution.py:369
  89.7 270.8 %all-to-all-start.1 = ((bf16[8,128,3840]{2,1,0:T(8,128)(2,1)}), bf16[8,128,3840]{2,1,0:T(8,128)(2,1)}, u32[]{:S(2)}, u32[]{:S(2)}) async-start(bf16[8,128,3840]{2,1,0:T(8,128)(2,1)} %param.9), calls=%async_computation.1 | async-start | bytes 15728640 | tf_op jit(solution)/shard_map/all_to_all | solution.py:369
  223.5 96.6 %copy-start.8 = (f32[3840]{0:T(1024)S(1)}, f32[3840]{0:T(1024)}, u32[]{:S(2)}) copy-start(f32[3840]{0:T(1024)} %get-tuple-element.60) | copy-start | bytes 46084
  434.5 97.8 %copy-start.5 = (f32[8,2,1024]{2,1,0:T(2,128)S(1)}, f32[8,2,1024]{2,1,0:T(2,128)}, u32[]{:S(2)}) copy-start(f32[8,2,1024]{2,1,0:T(2,128)} %get-tuple-element.53) | copy-start | bytes 196612
  434.5 99.0 %copy-start.1 = (f32[8,8192]{1,0:T(8,128)S(1)}, f32[8,8192]{1,0:T(8,128)}, u32[]{:S(2)}) copy-start(f32[8,8192]{1,0:T(8,128)} %get-tuple-element.50) | copy-start | bytes 786436
  543.7 92.1 %all-to-all-start.2 = ((bf16[8,128,3840]{2,1,0:T(8,128)(2,1)}), bf16[8,128,3840]{2,1,0:T(8,128)(2,1)}, u32[]{:S(2)}, u32[]{:S(2)}) async-start(bf16[8,128,3840]{2,1,0:T(8,128)(2,1)} %bitcast.64), calls=%async_computation.2 | async-start | bytes 15728640 | tf_op jit(solution)/shard_map/all_to_all | solution.py:369
  700.5 98.5 %copy-start.4 = (f32[8,2,1024]{2,1,0:T(2,128)S(1)}, f32[8,2,1024]{2,1,0:T(2,128)}, u32[]{:S(2)}) copy-start(f32[8,2,1024]{2,1,0:T(2,128)} %get-tuple-element.58) | copy-start | bytes 196612
  700.5 98.7 %copy-start = (f32[8,8192]{1,0:T(8,128)S(1)}, f32[8,8192]{1,0:T(8,128)}, u32[]{:S(2)}) copy-start(f32[8,8192]{1,0:T(8,128)} %get-tuple-element.56) | copy-start | bytes 786436
  809.1 10.8 %slice-start = ((f32[15888]{0:T(1024)}), f32[8192]{0:T(1024)S(1)}, s32[]{:S(2)}) async-start(f32[15888]{0:T(1024)} %reduce_sum.46), calls=%async_computation.6 | async-start | bytes 65536 | tf_op jit(solution)/shard_map/slice | solution.py:407
  809.1 10.8 %copy-start.2 = (f32[15888]{0:T(1024)S(1)}, f32[15888]{0:T(1024)}, u32[]{:S(2)}) copy-start(f32[15888]{0:T(1024)} %reduce_sum.46) | copy-start | bytes 190660
  809.1 92.2 %all-to-all-start.4 = ((bf16[8,128,3840]{2,1,0:T(8,128)(2,1)}), bf16[8,128,3840]{2,1,0:T(8,128)(2,1)}, u32[]{:S(2)}, u32[]{:S(2)}) async-start(bf16[8,128,3840]{2,1,0:T(8,128)(2,1)} %bitcast.63), calls=%async_computation.4 | async-start | bytes 15728640 | tf_op jit(solution)/shard_map/all_to_all | solution.py:369
